TPU v7x, 512 devices: a whole 4x8x8 slice. The times are simulated.
512 devices in a mesh: mode: 32 (over z_hi, y), space: 16 (over x, z_lo, core).
Axes of the slice: x: 4, y: 8, z: 8 (z_hi: 4, z_lo: 2; z = z_hi * 2 + z_lo), core: 2. Of those that a mesh axis runs over, the one named last changes fastest.
Arguments:
- pressure: float32 [512, 32, 4, 128], P('mode', 'space'), may hold values from -6 to 6
- source: float32 [512, 32, 4, 128], P('mode', 'space'), may hold values from -6 to 6
- coefficients: float32 [32, 32, 4, 128], P(None, 'space'), may hold values from 0.2 to 2
- coupling: float32 [32, 512, 512], P(None, 'mode'), as said below
Outputs:
- pressure_out: float32 [512, 32, 4, 128], P('mode', 'space')
- residual: float32 [512, 32, 4, 128], P('mode', 'space')
Inputs may be any that keep to these rules, and one draw needn't show every extreme that they name: coupling[k] is symmetric for every k.
All inputs are finite; a program needn't handle non-finite values.
Results may differ from a plain program's by a relative error of at most 0.00011.
Values sent between devices are 32-bit elements; how exact they have to be, the bound alone decides.
A program may use at most 64 MiB of HBM per device.

v0:
```python
import jax
import jax.numpy as jnp
from jax import lax
from jax.sharding import Mesh
from jax.sharding import PartitionSpec as P

ITERS = 2
MODE = ("mode_0", "mode_1")


storage_coef = 1.0
damping = 0.7


def extended(x, sides, width):
    for axis, dim in sides:
        devices, length = (lax.axis_size(axis), x.shape[dim])
        up = [(i, (i + 1) % devices) for i in range(devices - 1)]
        down = [(j, i) for i, j in up]
        last = lax.slice_in_dim(x, length - width, length, axis=dim)
        initial = lax.slice_in_dim(x, 0, width, axis=dim)
        before = lax.ppermute(last, axis, up)
        after = lax.ppermute(initial, axis, down)
        x = jnp.concatenate([before, x, after], axis=dim)
    return x


def own_block(pieces, axes, turns):
    inside = pieces.shape[1:]
    pieces = pieces.reshape(*(lax.axis_size(a) for a in axes), *inside)
    pieces = jnp.moveaxis(pieces, turns, range(len(axes))).reshape(-1, *inside)
    for k in turns:
        pieces = lax.psum_scatter(pieces, axes[k], scatter_dimension=0, tiled=True)
    return pieces[0]


def in_blocks(x, dim, devices):
    dims = x.shape
    pieces = x.reshape(*dims[:dim], devices, dims[dim] // devices, *dims[dim + 1 :])
    return jnp.moveaxis(pieces, dim, 0)


def sum_by_axis(x, axes, turns, dim):
    devices = lax.axis_size(axes)
    return own_block(in_blocks(x, dim, devices), axes, turns)


def shifted(padded, spatial_axis, offset):
    index = [slice(None)] * padded.ndim
    for place in (-3, -2, -1):
        index[place] = slice(1, padded.shape[place] - 1)
    index[spatial_axis] = slice(1 + offset, padded.shape[spatial_axis] - 1 + offset)
    return padded[tuple(index)]


def yz_pad(array):
    return jnp.pad(array, [(0, 0)] * (array.ndim - 2) + [(1, 1), (1, 1)])


def local_stencil(coef_x, field_x):
    coef_p = yz_pad(coef_x)
    field_p = yz_pad(field_x)
    centre_c = shifted(coef_p, -3, 0)
    centre_f = shifted(field_p, -3, 0)
    total = None
    for spatial_axis in (-3, -2, -1):
        for offset in (-1, 1):
            term = (
                0.5
                * (centre_c + shifted(coef_p, spatial_axis, offset))
                * (centre_f - shifted(field_p, spatial_axis, offset))
            )
            total = term if total is None else total + term
    return total


def face_total(coef_x):
    coef_p = yz_pad(coef_x)
    centre_c = shifted(coef_p, -3, 0)
    total = jnp.zeros(centre_c.shape, jnp.float32)
    for spatial_axis in (-3, -2, -1):
        for offset in (-1, 1):
            total = total + 0.5 * (centre_c + shifted(coef_p, spatial_axis, offset))
    return total


def on_device(pressure, source, coefficients, coupling):
    coef_x = extended(coefficients, (("space", 1),), 1)
    mean_x = coef_x[0]
    diag = storage_coef + face_total(mean_x)
    residual = source
    for outer in range(ITERS):
        own_x = extended(pressure, (("space", 1),), 1)
        worked = local_stencil(coef_x[:, None], own_x[None])
        applied = sum_by_axis(
            jnp.einsum("kji,kjxyz->ixyz", coupling, worked, precision=lax.Precision.HIGHEST),
            MODE,
            (1, 0),
            0,
        )
        residual = source - storage_coef * pressure - applied
        first = damping * residual / diag
        first_x = extended(first, (("space", 1),), 1)
        mean_apply = storage_coef * first + local_stencil(mean_x[None], first_x)
        second = first + damping * (residual - mean_apply) / diag
        pressure = pressure + second
    return (pressure, residual)


def solution(mesh):
    split = Mesh(mesh.devices.reshape(4, 8, mesh.shape["space"]), ("mode_0", "mode_1", "space"))
    in_specs = (
        P(MODE, "space", None, None),
        P(MODE, "space", None, None),
        P(None, "space", None, None),
        P(None, MODE, None),
    )
    out_specs = (P(MODE, "space", None, None), P(MODE, "space", None, None))
    return jax.shard_map(
        on_device, mesh=split, in_specs=in_specs, out_specs=out_specs, check_vma=False
    )
```

profile of v0, /device:TPU:1, one launch (start us, length us, event | category | flops | bytes accessed | tf_op | source)
XLA Modules:
  0.0 236.9 jit_solution(14768704335036836630)
XLA Ops:
  7.2 0.9 fusion.159
  8.1 5.4 %collective-permute-start.2 = (f32[16,1,4,128]{3,2,1,0:T(4,128)S(1)}, f32[16,1,4,128]{3,2,1,0:T(4,128)S(1)}, u32[]{:S(2)}, u32[]{:S(2)}) collective-permute-start(f32[16,1,4,128]{3,2,1,0:T(4,128)S(1)} %get-tuple-element.46), channel_id=1, source_target_pairs={{0,1},{1,2},{2,3},{3,4},{4,5},{5,6},{6,7},{7,8},{8,9},{9,10},{10,1... | collective-permute-start | bytes 98312 | tf_op jit(solution)/shard_map/ppermute | solution.py:22
  13.5 4.7 %collective-permute-start.3 = (f32[16,1,4,128]{3,2,1,0:T(4,128)S(1)}, f32[16,1,4,128]{3,2,1,0:T(4,128)S(1)}, u32[]{:S(2)}, u32[]{:S(2)}) collective-permute-start(f32[16,1,4,128]{3,2,1,0:T(4,128)S(1)} %get-tuple-element.47), channel_id=1, source_target_pairs={{1,0},{2,1},{3,2},{4,3},{5,4},{6,5},{7,6},{8,7},{9,8},{10,9},{11,1... | collective-permute-start | bytes 98312 | tf_op jit(solution)/shard_map/ppermute | solution.py:23
  18.2 0.9 fusion.155
  19.0 1.9 collective-permute-start.1
  21.0 3.6 %collective-permute-start = (f32[32,1,4,128]{3,2,1,0:T(4,128)S(1)}, f32[32,1,4,128]{3,2,1,0:T(4,128)S(1)}, u32[]{:S(2)}, u32[]{:S(2)}) collective-permute-start(f32[32,1,4,128]{3,2,1,0:T(4,128)S(1)} %get-tuple-element.39), channel_id=1, source_target_pairs={{0,1},{1,2},{2,3},{3,4},{4,5},{5,6},{6,7},{7,8},{8,9},{9,10},{10,1... | collective-permute-start | bytes 196616 | tf_op jit(solution)/shard_map/ppermute | solution.py:22
  24.6 0.9 maximum_bitcast_fusion
  26.0 0.5 copy-done.7
  27.8 5.9 %fusion.24 = f32[512,2,4,128]{0,3,2,1:T(8,128)} fusion(f32[16,2,4,128]{3,0,2,1:T(8,128)S(1)} %copy.63, f32[32,2,4,128]{3,0,2,1:T(8,128)S(1)} %copy.62, f32[16,2,4,128]{3,0,2,1:T(8,128)S(1)} %copy.61, f32[32,2,4,128]{3,0,2,1:T(8,128)S(1)} %copy.60, f32[16,2,4,128]{3,0,2,1:T(8,128)S(1)} %copy.59, f32[32,2,4,128]{3,0,2,1:T(8,128)S(1)} %copy.58, ...), kind=kOutput, calls=%fused_computation.28 | convolution fusion | flops 3226992640 | bytes 4325376 | tf_op jit(solution)/shard_map/kji,kjxyz->ixyz/dot_general | solution.py:96
  33.7 1.9 copy.65
  35.7 1.7 copy.66
  37.5 43.7 %reduce-scatter.5.cloned.1.call-done = f32[4,16,2,4,128]{4,1,3,2,0:T(8,128)} async-done(((f32[32,16,2,4,128]{4,1,3,2,0:T(8,128)}), f32[4,16,2,4,128]{4,1,3,2,0:T(8,128)}) %reduce-scatter.5.cloned.1.call-update) | async-done | bytes 262160 | tf_op jit(solution)/shard_map/reduce_scatter | solution.py:33
  81.5 33.3 %reduce-scatter.7.cloned.1.call-done = f32[1,16,2,4,128]{4,1,3,2,0:T(8,128)} async-done(((f32[4,16,2,4,128]{4,1,3,2,0:T(8,128)}), f32[1,16,2,4,128]{4,1,3,2,0:T(8,128)}) %reduce-scatter.7.cloned.1.call-update) | async-done | bytes 65552 | tf_op jit(solution)/shard_map/reduce_scatter | solution.py:33
  114.8 0.9 multiply_divide_fusion.1
  115.6 5.2 %collective-permute-start.4 = (f32[16,1,4,128]{3,0,2,1:T(8,128)S(1)}, f32[16,1,4,128]{3,0,2,1:T(8,128)S(1)}, u32[]{:S(2)}, u32[]{:S(2)}) collective-permute-start(f32[16,1,4,128]{3,0,2,1:T(8,128)S(1)} %get-tuple-element.44), channel_id=1, source_target_pairs={{0,1},{1,2},{2,3},{3,4},{4,5},{5,6},{6,7},{7,8},{8,9},{9,10},{10,1... | collective-permute-start | bytes 98312 | tf_op jit(solution)/shard_map/ppermute | solution.py:22
  120.8 1.9 collective-permute-start.5
  122.7 3.3 %collective-permute-done.5 = f32[16,1,4,128]{3,0,2,1:T(8,128)S(1)} collective-permute-done((f32[16,1,4,128]{3,0,2,1:T(8,128)S(1)}, f32[16,1,4,128]{3,0,2,1:T(8,128)S(1)}, u32[]{:S(2)}, u32[]{:S(2)}) %collective-permute-start.5) | collective-permute-done | bytes 32800 | tf_op jit(solution)/shard_map/ppermute | solution.py:23
  126.2 1.0 fusion.119
  127.2 1.9 collective-permute-start.6
  129.1 2.6 %collective-permute-start.7 = (f32[16,1,4,128]{3,0,2,1:T(8,128)S(1)}, f32[16,1,4,128]{3,0,2,1:T(8,128)S(1)}, u32[]{:S(2)}, u32[]{:S(2)}) collective-permute-start(f32[16,1,4,128]{3,0,2,1:T(8,128)S(1)} %get-tuple-element.43), channel_id=1, source_target_pairs={{1,0},{2,1},{3,2},{4,3},{5,4},{6,5},{7,6},{8,7},{9,8},{10,9},{11,1... | collective-permute-start | bytes 98312 | tf_op jit(solution)/shard_map/ppermute | solution.py:23
  131.7 4.2 %collective-permute-done.7 = f32[16,1,4,128]{3,0,2,1:T(8,128)S(1)} collective-permute-done((f32[16,1,4,128]{3,0,2,1:T(8,128)S(1)}, f32[16,1,4,128]{3,0,2,1:T(8,128)S(1)}, u32[]{:S(2)}, u32[]{:S(2)}) %collective-permute-start.7) | collective-permute-done | bytes 32800 | tf_op jit(solution)/shard_map/ppermute | solution.py:23
  136.1 5.9 %fusion.27 = f32[512,2,4,128]{0,3,2,1:T(8,128)} fusion(f32[16,2,4,128]{3,0,2,1:T(8,128)S(1)} %get-tuple-element.24, f32[16,2,4,128]{3,0,2,1:T(8,128)S(1)} %get-tuple-element.23, f32[16,2,4,128]{3,0,2,1:T(8,128)S(1)} %get-tuple-element.27, f32[16,2,4,128]{3,0,2,1:T(8,128)S(1)} %get-tuple-element.25, f32[16,2,4,128]{3,0,2,1:T(8,128)S(1)} %get-tuple-element.26, ...), kind=kOutput, calls=%fused_computation.29 | convolution fusion | flops 3226992640 | bytes 4325376 | tf_op jit(solution)/shard_map/kji,kjxyz->ixyz/dot_general | solution.py:96
  142.0 1.9 copy.70
  143.9 1.7 copy.71
  145.7 39.5 %reduce-scatter.9.cloned.1.call-done = f32[4,16,2,4,128]{4,1,3,2,0:T(8,128)} async-done(((f32[32,16,2,4,128]{4,1,3,2,0:T(8,128)}), f32[4,16,2,4,128]{4,1,3,2,0:T(8,128)}) %reduce-scatter.9.cloned.1.call-update) | async-done | bytes 262160 | tf_op jit(solution)/shard_map/reduce_scatter | solution.py:33
  185.2 33.0 %reduce-scatter.11.cloned.1.call-done = f32[1,16,2,4,128]{4,1,3,2,0:T(8,128)} async-done(((f32[4,16,2,4,128]{4,1,3,2,0:T(8,128)}), f32[1,16,2,4,128]{4,1,3,2,0:T(8,128)}) %reduce-scatter.11.cloned.1.call-update) | async-done | bytes 65552 | tf_op jit(solution)/shard_map/reduce_scatter | solution.py:33
  218.2 0.9 multiply_divide_fusion
  219.1 5.1 %collective-permute-start.8 = (f32[16,1,4,128]{3,0,2,1:T(8,128)S(1)}, f32[16,1,4,128]{3,0,2,1:T(8,128)S(1)}, u32[]{:S(2)}, u32[]{:S(2)}) collective-permute-start(f32[16,1,4,128]{3,0,2,1:T(8,128)S(1)} %get-tuple-element.40), channel_id=1, source_target_pairs={{0,1},{1,2},{2,3},{3,4},{4,5},{5,6},{6,7},{7,8},{8,9},{9,10},{10,1... | collective-permute-start | bytes 98312 | tf_op jit(solution)/shard_map/ppermute | solution.py:22
  224.2 1.9 collective-permute-start.9
  226.2 0.7 copy.73
  226.8 2.6 %collective-permute-done.9 = f32[16,1,4,128]{3,0,2,1:T(8,128)S(1)} collective-permute-done((f32[16,1,4,128]{3,0,2,1:T(8,128)S(1)}, f32[16,1,4,128]{3,0,2,1:T(8,128)S(1)}, u32[]{:S(2)}, u32[]{:S(2)}) %collective-permute-start.9) | collective-permute-done | bytes 32800 | tf_op jit(solution)/shard_map/ppermute | solution.py:23
  229.7 0.7 copy.72
  (84 shorter events, 2.5 us)
Async XLA Ops:
  7.2 20.0 %copy-start = (f32[32,16,512]{2,1,0:T(8,128)S(1)}, f32[32,16,512]{2,1,0:T(8,128)}, u32[]{:S(2)}) copy-start(f32[32,16,512]{2,1,0:T(8,128)} %param.7) | copy-start | bytes 3145732
  7.2 18.8 %copy-start.1 = (f32[32,2,4,128]{3,2,1,0:T(4,128)S(1)}, f32[32,2,4,128]{3,2,1,0:T(4,128)}, u32[]{:S(2)}) copy-start(f32[32,2,4,128]{3,2,1,0:T(4,128)} %param.6) | copy-start | bytes 393220
  7.2 74.0 %reduce-scatter.5.cloned.1.call-start = ((), (), s32[]{:S(2)}) async-start(), calls=%async_computation.4 | async-start | bytes 2359296 | tf_op jit(solution)/shard_map/reduce_scatter | solution.py:33
  8.1 16.5 %collective-permute-start.2 = (f32[16,1,4,128]{3,2,1,0:T(4,128)S(1)}, f32[16,1,4,128]{3,2,1,0:T(4,128)S(1)}, u32[]{:S(2)}, u32[]{:S(2)}) collective-permute-start(f32[16,1,4,128]{3,2,1,0:T(4,128)S(1)} %get-tuple-element.46), channel_id=1, source_target_pairs={{0,1},{1,2},{2,3},{3,4},{4,5},{5,6},{6,7},{7,8},{8,9},{9,10},{10,1... | collective-permute-start | bytes 98312 | tf_op jit(solution)/shard_map/ppermute | solution.py:22
  13.5 11.1 %collective-permute-start.3 = (f32[16,1,4,128]{3,2,1,0:T(4,128)S(1)}, f32[16,1,4,128]{3,2,1,0:T(4,128)S(1)}, u32[]{:S(2)}, u32[]{:S(2)}) collective-permute-start(f32[16,1,4,128]{3,2,1,0:T(4,128)S(1)} %get-tuple-element.47), channel_id=1, source_target_pairs={{1,0},{2,1},{3,2},{4,3},{5,4},{6,5},{7,6},{8,7},{9,8},{10,9},{11,1... | collective-permute-start | bytes 98312 | tf_op jit(solution)/shard_map/ppermute | solution.py:23
  19.0 6.9 %collective-permute-start.1 = (f32[32,1,4,128]{3,2,1,0:T(4,128)S(1)}, f32[32,1,4,128]{3,2,1,0:T(4,128)S(1)}, u32[]{:S(2)}, u32[]{:S(2)}) collective-permute-start(f32[32,1,4,128]{3,2,1,0:T(4,128)S(1)} %get-tuple-element.38), channel_id=1, source_target_pairs={{1,0},{2,1},{3,2},{4,3},{5,4},{6,5},{7,6},{8,7},{9,8},{10,9},{11,1... | collective-permute-start | bytes 196616 | tf_op jit(solution)/shard_map/ppermute | solution.py:23
  21.0 5.0 %collective-permute-start = (f32[32,1,4,128]{3,2,1,0:T(4,128)S(1)}, f32[32,1,4,128]{3,2,1,0:T(4,128)S(1)}, u32[]{:S(2)}, u32[]{:S(2)}) collective-permute-start(f32[32,1,4,128]{3,2,1,0:T(4,128)S(1)} %get-tuple-element.39), channel_id=1, source_target_pairs={{0,1},{1,2},{2,3},{3,4},{4,5},{5,6},{6,7},{7,8},{8,9},{9,10},{10,1... | collective-permute-start | bytes 196616 | tf_op jit(solution)/shard_map/ppermute | solution.py:22
  26.9 0.7 copy-start.9
  27.0 0.7 copy-start.13
  27.0 0.7 copy-start.15
  27.1 0.7 copy-start.17
  27.1 0.7 copy-start.19
  37.3 44.0 %copy-start.6 = (f32[32,1,4,128]{3,2,1,0:T(4,128)S(1)}, f32[32,1,4,128]{3,2,1,0:T(4,128)}, u32[]{:S(2)}) copy-start(f32[32,1,4,128]{3,2,1,0:T(4,128)} %copy-done.5) | copy-start | bytes 196612
  37.3 44.0 %copy-start.8 = (f32[32,1,4,128]{3,2,1,0:T(4,128)S(1)}, f32[32,1,4,128]{3,2,1,0:T(4,128)}, u32[]{:S(2)}) copy-start(f32[32,1,4,128]{3,2,1,0:T(4,128)} %copy-done.7) | copy-start | bytes 196612
  37.3 77.4 %copy-start.2 = (f32[16,2,4,128]{3,2,1,0:T(4,128)S(1)}, f32[16,2,4,128]{3,2,1,0:T(4,128)}, u32[]{:S(2)}) copy-start(f32[16,2,4,128]{3,2,1,0:T(4,128)} %param.4) | copy-start | bytes 196612
  37.3 77.4 %copy-start.3 = (f32[16,2,4,128]{3,2,1,0:T(4,128)S(1)}, f32[16,2,4,128]{3,2,1,0:T(4,128)}, u32[]{:S(2)}) copy-start(f32[16,2,4,128]{3,2,1,0:T(4,128)} %param.5) | copy-start | bytes 196612
  37.4 98.7 %copy-start.10 = (f32[32,2,4,128]{3,0,2,1:T(8,128)S(1)}, f32[32,2,4,128]{3,0,2,1:T(8,128)}, u32[]{:S(2)}) copy-start(f32[32,2,4,128]{3,0,2,1:T(8,128)} %copy-done.9) | copy-start | bytes 393220
  37.4 98.7 %copy-start.12 = (f32[32,2,4,128]{3,0,2,1:T(8,128)S(1)}, f32[32,2,4,128]{3,0,2,1:T(8,128)}, u32[]{:S(2)}) copy-start(f32[32,2,4,128]{3,0,2,1:T(8,128)} %copy-done.11) | copy-start | bytes 393220
  37.4 98.7 %copy-start.14 = (f32[32,2,4,128]{3,0,2,1:T(8,128)S(1)}, f32[32,2,4,128]{3,0,2,1:T(8,128)}, u32[]{:S(2)}) copy-start(f32[32,2,4,128]{3,0,2,1:T(8,128)} %copy-done.13) | copy-start | bytes 393220
  37.4 98.7 %copy-start.16 = (f32[32,2,4,128]{3,0,2,1:T(8,128)S(1)}, f32[32,2,4,128]{3,0,2,1:T(8,128)}, u32[]{:S(2)}) copy-start(f32[32,2,4,128]{3,0,2,1:T(8,128)} %copy-done.15) | copy-start | bytes 393220
  37.4 98.7 %copy-start.18 = (f32[32,2,4,128]{3,0,2,1:T(8,128)S(1)}, f32[32,2,4,128]{3,0,2,1:T(8,128)}, u32[]{:S(2)}) copy-start(f32[32,2,4,128]{3,0,2,1:T(8,128)} %copy-done.17) | copy-start | bytes 393220
  37.4 98.7 %copy-start.20 = (f32[32,2,4,128]{3,0,2,1:T(8,128)S(1)}, f32[32,2,4,128]{3,0,2,1:T(8,128)}, u32[]{:S(2)}) copy-start(f32[32,2,4,128]{3,0,2,1:T(8,128)} %copy-done.19) | copy-start | bytes 393220
  37.4 77.3 %reduce-scatter.7.cloned.1.call-start = ((), (), s32[]{:S(2)}) async-start(), calls=%async_computation.5 | async-start | bytes 327680 | tf_op jit(solution)/shard_map/reduce_scatter | solution.py:33
  81.2 104.0 %reduce-scatter.9.cloned.1.call-start = ((), (), s32[]{:S(2)}) async-start(), calls=%async_computation.6 | async-start | bytes 2359296 | tf_op jit(solution)/shard_map/reduce_scatter | solution.py:33
  115.6 7.1 %collective-permute-start.4 = (f32[16,1,4,128]{3,0,2,1:T(8,128)S(1)}, f32[16,1,4,128]{3,0,2,1:T(8,128)S(1)}, u32[]{:S(2)}, u32[]{:S(2)}) collective-permute-start(f32[16,1,4,128]{3,0,2,1:T(8,128)S(1)} %get-tuple-element.44), channel_id=1, source_target_pairs={{0,1},{1,2},{2,3},{3,4},{4,5},{5,6},{6,7},{7,8},{8,9},{9,10},{10,1... | collective-permute-start | bytes 98312 | tf_op jit(solution)/shard_map/ppermute | solution.py:22
  120.8 5.2 %collective-permute-start.5 = (f32[16,1,4,128]{3,0,2,1:T(8,128)S(1)}, f32[16,1,4,128]{3,0,2,1:T(8,128)S(1)}, u32[]{:S(2)}, u32[]{:S(2)}) collective-permute-start(f32[16,1,4,128]{3,0,2,1:T(8,128)S(1)} %get-tuple-element.45), channel_id=1, source_target_pairs={{1,0},{2,1},{3,2},{4,3},{5,4},{6,5},{7,6},{8,7},{9,8},{10,9},{11,1... | collective-permute-start | bytes 98312 | tf_op jit(solution)/shard_map/ppermute | solution.py:23
  127.2 4.5 %collective-permute-start.6 = (f32[16,1,4,128]{3,0,2,1:T(8,128)S(1)}, f32[16,1,4,128]{3,0,2,1:T(8,128)S(1)}, u32[]{:S(2)}, u32[]{:S(2)}) collective-permute-start(f32[16,1,4,128]{3,0,2,1:T(8,128)S(1)} %get-tuple-element.42), channel_id=1, source_target_pairs={{0,1},{1,2},{2,3},{3,4},{4,5},{5,6},{6,7},{7,8},{8,9},{9,10},{10,1... | collective-permute-start | bytes 98312 | tf_op jit(solution)/shard_map/ppermute | solution.py:22
  129.1 6.8 %collective-permute-start.7 = (f32[16,1,4,128]{3,0,2,1:T(8,128)S(1)}, f32[16,1,4,128]{3,0,2,1:T(8,128)S(1)}, u32[]{:S(2)}, u32[]{:S(2)}) collective-permute-start(f32[16,1,4,128]{3,0,2,1:T(8,128)S(1)} %get-tuple-element.43), channel_id=1, source_target_pairs={{1,0},{2,1},{3,2},{4,3},{5,4},{6,5},{7,6},{8,7},{9,8},{10,9},{11,1... | collective-permute-start | bytes 98312 | tf_op jit(solution)/shard_map/ppermute | solution.py:23
  145.6 72.6 %copy-start.4 = (f32[16,2,4,128]{3,2,1,0:T(4,128)S(1)}, f32[16,2,4,128]{3,2,1,0:T(4,128)}, u32[]{:S(2)}) copy-start(f32[16,2,4,128]{3,2,1,0:T(4,128)} %param.5) | copy-start | bytes 196612
  145.6 72.6 %reduce-scatter.11.cloned.1.call-start = ((), (), s32[]{:S(2)}) async-start(), calls=%async_computation.7 | async-start | bytes 327680 | tf_op jit(solution)/shard_map/reduce_scatter | solution.py:33
  219.1 7.7 %collective-permute-start.8 = (f32[16,1,4,128]{3,0,2,1:T(8,128)S(1)}, f32[16,1,4,128]{3,0,2,1:T(8,128)S(1)}, u32[]{:S(2)}, u32[]{:S(2)}) collective-permute-start(f32[16,1,4,128]{3,0,2,1:T(8,128)S(1)} %get-tuple-element.40), channel_id=1, source_target_pairs={{0,1},{1,2},{2,3},{3,4},{4,5},{5,6},{6,7},{7,8},{8,9},{9,10},{10,1... | collective-permute-start | bytes 98312 | tf_op jit(solution)/shard_map/ppermute | solution.py:22
  224.2 5.2 %collective-permute-start.9 = (f32[16,1,4,128]{3,0,2,1:T(8,128)S(1)}, f32[16,1,4,128]{3,0,2,1:T(8,128)S(1)}, u32[]{:S(2)}, u32[]{:S(2)}) collective-permute-start(f32[16,1,4,128]{3,0,2,1:T(8,128)S(1)} %get-tuple-element.41), channel_id=1, source_target_pairs={{1,0},{2,1},{3,2},{4,3},{5,4},{6,5},{7,6},{8,7},{9,8},{10,9},{11,1... | collective-permute-start | bytes 98312 | tf_op jit(solution)/shard_map/ppermute | solution.py:23
  (3 other events, 1.9 us)
Sparse Core Ops, SparseCore 0:
  37.5 43.6 reduce-scatter.4
  84.0 30.6 reduce-scatter.6
  145.7 39.4 reduce-scatter.8
  187.9 30.3 reduce-scatter.10
where the time goes:
time: 238 us; the launch traced here: 237 us
  waiting for transfers between devices  160 us (67%)
  starting transfers between devices  34.4 us (14%)
  between operations  14.3 us (6%)
  local copies, waits for them, and re-layouts  11.9 us (5%)
  matrix products  11.9 us (5%)
  other arithmetic  4.63 us (2%)
    reduce_scatter x4, waiting for transfers between devices, own_block(): pieces = lax.psum_scatter(pieces, axes[k], scatter_dimension=0, tiled=True)  150 us
    ppermute x5, starting transfers between devices, extended(): before = lax.ppermute(last, axis, up)  21.2 us
    ppermute x5, starting transfers between devices, extended(): after = lax.ppermute(initial, axis, down)  13 us
    dot_general x2, matrix products, on_device(): jnp.einsum('kji,kjxyz->ixyz', coupling, worked, precision=lax.Precision.H...  11.9 us
    ppermute x5, waiting for transfers between devices, extended(): after = lax.ppermute(initial, axis, down)  10.2 us
  transfers between devices with their start and end apart: 14, of which 8 were waited for; matrix products, arithmetic and copies ran while one was open for 1% of the time, Pallas kernels for 0%

commit v1 on v0

v1 whole, which is shorter than its diff:
```python
import functools

import jax
import jax.numpy as jnp
from jax import lax
from jax.experimental import pallas as pl
from jax.experimental.pallas import tpu as pltpu
from jax.sharding import PartitionSpec as P

MESH = pl.DeviceIdType.MESH
ITERS = 2
DAMP = 0.7
KT, IB, PM = 32, 16, 512
NY, NZ = 8, 4
CELLS = 1024
SPLIT = 768
F32, BF16 = jnp.float32, jnp.bfloat16

AZ = 0
AR = AZ + 3
AL = AR + 16
BR = AL + 16
BL = BR + 4
BZ = BL + 4
NMSG = BZ + 24


def lanes_next(v):
    n = v.shape[-1]
    lane = lax.broadcasted_iota(jnp.int32, v.shape, v.ndim - 1)
    return jnp.where(lane < n - 1, pltpu.roll(v, n - 1, v.ndim - 1), 0.0)


def lanes_prev(v):
    lane = lax.broadcasted_iota(jnp.int32, v.shape, v.ndim - 1)
    return jnp.where(lane > 0, pltpu.roll(v, 1, v.ndim - 1), 0.0)


def split_bf16(x):
    hi = x.astype(BF16)
    return hi, (x - hi.astype(F32)).astype(BF16)


def kernel(u_ref, src_ref, a_ref, c_ref, po_ref, ro_ref,
           ug, a_halo, c_hi, c_lo, faces, dinv, m_ref, uh_ref, ul_ref,
           hs_send, hs_recv, out_u, src_m,
           gs, gr, hss, hsr, cs, cr):
    mode, space = lax.axis_index("mode"), lax.axis_index("space")
    ns = lax.axis_size("space")
    zh, y = mode // NY, lax.rem(mode, NY)
    left_s, right_s = lax.rem(space + ns - 1, ns), lax.rem(space + 1, ns)
    yr = zh * NY + lax.rem(y + 1, NY)
    yl = zh * NY + lax.rem(y + NY - 1, NY)

    def at_z(q):
        return lax.rem(zh + q, NZ) * NY + y

    def block(q, d):
        return lax.rem(zh + q, NZ) * NY + lax.rem(y + NY + d, NY)

    barrier = pltpu.get_barrier_semaphore()
    for target in (yr, yl, at_z(1), at_z(2), at_z(3)):
        pl.semaphore_signal(barrier, inc=1, device_id={"mode": target, "space": space}, device_id_type=MESH)
    for target in (left_s, right_s):
        pl.semaphore_signal(barrier, inc=1, device_id={"mode": mode, "space": target}, device_id_type=MESH)

    for s in range(8):
        ug[0, mode, :, s * 128:(s + 1) * 128] = u_ref[:, s, :]
        src_m[:, s * 128:(s + 1) * 128] = src_ref[:, s, :]
    pl.semaphore_wait(barrier, 7)

    def coef_copy(side):
        target = right_s if side == 0 else left_s
        return pltpu.make_async_remote_copy(
            src_ref=a_ref, dst_ref=a_halo.at[side], send_sem=cs.at[side], recv_sem=cr.at[side],
            device_id={"mode": mode, "space": target}, device_id_type=MESH)

    def halo_copy(it, side):
        target = right_s if side == 0 else left_s
        return pltpu.make_async_remote_copy(
            src_ref=hs_send.at[it, side], dst_ref=hs_recv.at[it, side],
            send_sem=hss.at[it, side], recv_sem=hsr.at[it, side],
            device_id={"mode": mode, "space": target}, device_id_type=MESH)

    acols, bcols = slice(0, SPLIT), slice(SPLIT, CELLS)

    def gather(it):
        sent = []

        def msg(number, b, cols, target):
            return pltpu.make_async_remote_copy(
                src_ref=ug.at[it, b, :, cols], dst_ref=ug.at[it, b, :, cols],
                send_sem=gs.at[it, number], recv_sem=gr.at[it, number],
                device_id={"mode": target, "space": space}, device_id_type=MESH)

        def send(number, b, cols, target):
            copy = msg(number, b, cols, target)
            copy.start()
            sent.append(copy)

        def arrive(number, b, cols):
            msg(number, b, cols, yr).wait_recv()

        limit_r = [4, 3, 4, 3]
        limit_l = [3, 4, 3, 4]

        def a_right(q, t):
            send(AR + q * 4 + t - 1, block(q, -(t - 1)), acols, yr)

        def a_left(q, t):
            send(AL + q * 4 + t - 1, block(q, t - 1), acols, yl)

        def b_z(d):
            for q in (1, 2, 3):
                send(BZ + (d % NY) * 3 + q - 1, block(0, d), bcols, at_z(q))

        for q in (1, 3, 2):
            send(AZ + q - 1, mode, acols, at_z(q))
        send(BR + 0, mode, bcols, yr)
        send(BL + 0, mode, bcols, yl)
        a_right(0, 1)
        a_left(0, 1)
        b_z(0)
        for q in (1, 3, 2):
            arrive(AZ + q - 1, block(NZ - q, 0), acols)
            a_right(NZ - q, 1)
            a_left(NZ - q, 1)
        for t in (1, 2, 3, 4):
            if t <= 4:
                arrive(BR + t - 1, block(0, -t), bcols)
                if t < 4:
                    send(BR + t, block(0, -t), bcols, yr)
                b_z(-t)
            if t <= 3:
                arrive(BL + t - 1, block(0, t), bcols)
                if t < 3:
                    send(BL + t, block(0, t), bcols, yl)
                b_z(t)
            for q in (0, 3, 1, 2):
                if t <= limit_r[q]:
                    arrive(AR + q * 4 + t - 1, block(q, -t), acols)
                    if t < limit_r[q]:
                        a_right(q, t + 1)
                if t <= limit_l[q]:
                    arrive(AL + q * 4 + t - 1, block(q, t), acols)
                    if t < limit_l[q]:
                        a_left(q, t + 1)
        for d in range(NY):
            for q in (1, 2, 3):
                arrive(BZ + d * 3 + q - 1, block(NZ - q, d), bcols)
        return sent

    def prepare():
        for r in range(8):
            rows = slice(r * 64, (r + 1) * 64)
            hi, lo = split_bf16(c_ref[rows, :])
            c_hi[rows, :] = hi
            c_lo[rows, :] = lo
        coef_copy(0).wait_recv()
        coef_copy(1).wait_recv()
        sub = lax.broadcasted_iota(jnp.int32, (8, 128), 0)
        ysub = lax.rem(sub, 4)
        plane0 = sub < 4
        has_l, has_r = space > 0, space < ns - 1

        def one(k, _):
            a = a_ref[k]
            al = jnp.where(has_l, a_halo[0, k], 0.0)
            ar = jnp.where(has_r, a_halo[1, k], 0.0)
            a4 = pltpu.roll(a, 4, 0)
            xm = jnp.where(plane0, pltpu.roll(al, 4, 0), a4)
            xp = jnp.where(plane0, a4, pltpu.roll(ar, 4, 0))
            ym = jnp.where(ysub > 0, pltpu.roll(a, 1, 0), 0.0)
            yp = jnp.where(ysub < 3, pltpu.roll(a, 7, 0), 0.0)
            for n, v in enumerate((xm, xp, ym, yp, lanes_prev(a), lanes_next(a))):
                faces[n, k] = 0.5 * (a + v)
            return 0

        lax.fori_loop(0, KT, one, 0)

        def face_sum(a, x_nb):
            total = x_nb
            total = total + jnp.where(ysub > 0, pltpu.roll(a, 1, 0), 0.0)
            total = total + jnp.where(ysub < 3, pltpu.roll(a, 7, 0), 0.0)
            total = total + lanes_prev(a) + lanes_next(a)
            return 1.0 + 0.5 * (6.0 * a + total)

        a = a_ref[0]
        al = jnp.where(has_l, a_halo[0, 0], 0.0)
        ar = jnp.where(has_r, a_halo[1, 0], 0.0)
        a4, al4, ar4 = pltpu.roll(a, 4, 0), pltpu.roll(al, 4, 0), pltpu.roll(ar, 4, 0)
        dinv[0] = DAMP / face_sum(a, a4 + jnp.where(plane0, al4, ar4))
        dinv[1] = DAMP / face_sum(al, a4 + al4)
        dinv[2] = DAMP / face_sum(ar, a4 + ar4)

    def mixed(it):
        for r in range(8):
            x = ug[it, r * 4:(r + 1) * 4].reshape(64, CELLS)
            hi, lo = split_bf16(x)
            uh_ref[r * 64:(r + 1) * 64, :] = hi
            ul_ref[r * 64:(r + 1) * 64, :] = lo
        for t in range(4):
            cols = slice(t * 256, (t + 1) * 256)
            uh, ul = uh_ref[:, cols], ul_ref[:, cols]
            acc = jnp.dot(c_hi[...], uh, preferred_element_type=F32)
            acc += jnp.dot(c_hi[...], ul, preferred_element_type=F32)
            acc += jnp.dot(c_lo[...], uh, preferred_element_type=F32)
            m_ref[:, cols] = acc

    def sums(s):
        def one(k, acc):
            m = m_ref[pl.ds(pl.multiple_of(k * IB, IB), IB), s * 128:(s + 1) * 128]
            return tuple(acc[n] + faces[n, k, s:s + 1, :] * m for n in range(6))

        zero = jnp.zeros((IB, 128), F32)
        return lax.fori_loop(0, KT, one, (zero,) * 6, unroll=4)

    def tile(s):
        return slice(s * 128, (s + 1) * 128)

    coef_copy(0).start()
    coef_copy(1).start()
    sent = []
    has_l = space > 0
    has_r = space < ns - 1
    for it in range(ITERS):
        sent += gather(it)
        if it == 0:
            prepare()
        mixed(it)
        S = [sums(s) for s in range(8)]
        own = [ug[it, mode, :, tile(s)] for s in range(8)]
        part = []
        for s in range(8):
            xm, xp, ym, yp, zm, zp = S[s]
            ap = (xm + xp) + (ym + yp) + (zm + zp)
            ap = ap - (S[s + 4][0] if s < 4 else S[s - 4][1])
            if s % 4 < 3:
                ap = ap - S[s + 1][2]
            if s % 4 > 0:
                ap = ap - S[s - 1][3]
            ap = ap - lanes_next(zm) - lanes_prev(zp)
            part.append(src_m[:, tile(s)] - own[s] - ap)
        for c in range(4):
            hs_send[it, 0, :, tile(c)] = S[4 + c][1]
            hs_send[it, 0, :, tile(4 + c)] = part[4 + c]
            hs_send[it, 1, :, tile(c)] = S[c][0]
            hs_send[it, 1, :, tile(4 + c)] = part[c]
        halo_copy(it, 0).start()
        halo_copy(it, 1).start()
        halo_copy(it, 0).wait_recv()
        halo_copy(it, 1).wait_recv()
        res, first = [], []
        left_first, right_first = [], []
        for c in range(4):
            res.append(part[c] + jnp.where(has_l, hs_recv[it, 0, :, tile(c)], 0.0))
            v = (hs_recv[it, 0, :, tile(4 + c)] + S[c][0]) * dinv[1, 4 + c:5 + c, :]
            left_first.append(jnp.where(has_l, v, 0.0))
        for c in range(4):
            res.append(part[4 + c] + jnp.where(has_r, hs_recv[it, 1, :, tile(c)], 0.0))
            v = (hs_recv[it, 1, :, tile(4 + c)] + S[4 + c][1]) * dinv[2, c:c + 1, :]
            right_first.append(jnp.where(has_r, v, 0.0))
        for s in range(8):
            first.append(res[s] * dinv[0, s:s + 1, :])
        for s in range(8):
            f = first[s]
            fc = [faces[n, 0, s:s + 1, :] for n in range(6)]
            ap = f
            ap = ap + fc[0] * (f - (first[s - 4] if s >= 4 else left_first[s]))
            ap = ap + fc[1] * (f - (first[s + 4] if s < 4 else right_first[s - 4]))
            ap = ap + fc[2] * (f - first[s - 1] if s % 4 > 0 else f)
            ap = ap + fc[3] * (f - first[s + 1] if s % 4 < 3 else f)
            ap = ap + fc[4] * (f - lanes_prev(f))
            ap = ap + fc[5] * (f - lanes_next(f))
            second = f + (res[s] - ap) * dinv[0, s:s + 1, :]
            new = own[s] + second
            if it + 1 < ITERS:
                ug[it + 1, mode, :, tile(s)] = new
            else:
                po_ref[:, s, :] = new
                ro_ref[:, s, :] = res[s]
    for copy in sent:
        copy.wait_send()
    for side in (0, 1):
        coef_copy(side).wait_send()
        for it in range(ITERS):
            halo_copy(it, side).wait_send()


def on_device(pressure, source, coefficients, coupling):
    vmem = pl.BlockSpec(memory_space=pltpu.VMEM)
    shape = jax.ShapeDtypeStruct((IB, 8, 128), F32)
    dma = pltpu.SemaphoreType.DMA
    out = pl.pallas_call(
        kernel,
        out_shape=(shape, shape),
        in_specs=[vmem] * 4,
        out_specs=(vmem, vmem),
        scratch_shapes=[
            pltpu.VMEM((ITERS, PM // IB, IB, CELLS), F32),
            pltpu.VMEM((2, KT, 8, 128), F32),
            pltpu.VMEM((PM, PM), BF16),
            pltpu.VMEM((PM, PM), BF16),
            pltpu.VMEM((6, KT, 8, 128), F32),
            pltpu.VMEM((3, 8, 128), F32),
            pltpu.VMEM((PM, CELLS), F32),
            pltpu.VMEM((PM, CELLS), BF16),
            pltpu.VMEM((PM, CELLS), BF16),
            pltpu.VMEM((ITERS, 2, IB, CELLS), F32),
            pltpu.VMEM((ITERS, 2, IB, CELLS), F32),
            pltpu.VMEM((IB, CELLS), F32),
            pltpu.VMEM((IB, CELLS), F32),
            dma((ITERS, NMSG)),
            dma((ITERS, NMSG)),
            dma((ITERS, 2)),
            dma((ITERS, 2)),
            dma((2,)),
            dma((2,)),
        ],
        compiler_params=pltpu.CompilerParams(
            collective_id=0, has_side_effects=True, vmem_limit_bytes=40 * 1024 * 1024),
    )(pressure.reshape(IB, 8, 128), source.reshape(IB, 8, 128),
      coefficients.reshape(KT, 8, 128), coupling.reshape(PM, PM))
    return tuple(o.reshape(IB, 2, 4, 128) for o in out)


def solution(mesh):
    return jax.shard_map(
        on_device, mesh=mesh,
        in_specs=(P("mode", "space", None, None), P("mode", "space", None, None),
                  P(None, "space", None, None), P(None, "mode", None)),
        out_specs=(P("mode", "space", None, None), P("mode", "space", None, None)),
        check_vma=False)
```

time: 238 us -> 89.8 us (0.38)
  waiting for transfers between devices: 160 us -> 0 us
  Pallas kernels: 0 us -> 82.4 us
  starting transfers between devices: 34.4 us -> 0 us
  between operations: 14.3 us -> 0.65 us
  matrix products: 11.9 us -> 0 us
  local copies, waits for them, and re-layouts: 11.9 us -> 5.06 us
  other arithmetic: 4.63 us -> 0 us
    reduce_scatter x4 -> x0, waiting for transfers between devices: 150 us -> none  [own_block(): pieces = lax.psum_scatter(pieces, axes[k], scatter_dimension=0, tiled=True)]
    pallas_call x0 -> x1, Pallas kernels: none -> 82.4 us  [on_device(): pl.pallas_call(kernel, out_shape=(shape, shape), in_specs=[vmem] * 4, out...]
    ppermute x10 -> x0, starting transfers between devices: 34.2 us -> none  [the longest x5 21.2 us: extended(): before = lax.ppermute(last, axis, up)]
    dot_general x2 -> x0, matrix products: 11.9 us -> none  [on_device(): jnp.einsum('kji,kjxyz->ixyz', coupling, worked, precision=lax.Precision.H...]
    ppermute x10 -> x0, waiting for transfers between devices: 10.3 us -> none  [the longest x5 10.2 us: extended(): after = lax.ppermute(initial, axis, down)]
    dot_general x2 -> x0, local copies, waits for them, and re-layouts: 3.81 us -> none  [on_device(): jnp.einsum('kji,kjxyz->ixyz', coupling, worked, precision=lax.Precision.H...]
    transpose x2 -> x0, local copies, waits for them, and re-layouts: 3.35 us -> none  [own_block(): pieces = jnp.moveaxis(pieces, turns, range(len(axes))).reshape(-1, *inside)]
    unnamed x46 -> x10, local copies, waits for them, and re-layouts: 2.67 us -> 5.06 us
  transfers between devices with their start and end apart: 14 -> 0, of which waited for: 8 -> 0; matrix products, arithmetic and copies ran while one was open for 1% -> 0% of each run, Pallas kernels for 0% -> 0%
where the time goes in v1:
time: 89.8 us; the launch traced here: 88.1 us
  Pallas kernels  82.4 us (92%)
  local copies, waits for them, and re-layouts  5.06 us (6%)
    pallas_call x1, Pallas kernels, on_device(): pl.pallas_call(kernel, out_shape=(shape, shape), in_specs=[vmem] * 4, out...  82.4 us
    unnamed x10, local copies, waits for them, and re-layouts  5.06 us

profile of v1, /device:TPU:1, one launch (start us, length us, event | category | flops | bytes accessed | tf_op | source)
XLA Modules:
  0.0 88.1 jit_solution(8346210544177034869)
XLA Ops:
  0.6 0.0 copy-start
  0.6 1.2 %copy-done = f32[32,16,512]{2,1,0:T(8,128)S(1)} copy-done((f32[32,16,512]{2,1,0:T(8,128)S(1)}, f32[32,16,512]{2,1,0:T(8,128)}, u32[]{:S(2)}) %copy-start) | copy-done | bytes 1048600
  1.9 0.0 copy-start.1
  1.9 0.9 %copy-done.1 = f32[32,2,4,128]{3,2,1,0:T(4,128)S(1)} copy-done((f32[32,2,4,128]{3,2,1,0:T(4,128)S(1)}, f32[32,2,4,128]{3,2,1,0:T(4,128)}, u32[]{:S(2)}) %copy-start.1) | copy-done | bytes 131096
  2.8 0.0 copy-start.2
  2.8 0.8 copy-done.2
  3.6 0.0 copy-start.3
  3.6 0.8 copy-done.3
  4.4 82.4 %shard_map.59 = (f32[16,8,128]{2,1,0:T(8,128)S(1)}, f32[16,8,128]{2,1,0:T(8,128)S(1)}) custom-call(f32[16,8,128]{2,1,0:T(8,128)S(1)} %bitcast.8, f32[16,8,128]{2,1,0:T(8,128)S(1)} %bitcast.9, f32[32,8,128]{2,1,0:T(8,128)S(1)} %bitcast.7, f32[512,512]{1,0:T(8,128)S(1)} %bitcast.6), custom_call_target="tpu_custom_call" | custom-call | tf_op jit(solution)/shard_map/pallas_call | solution.py:294
  86.9 0.6 copy.8
  87.5 0.6 copy.9
Async XLA Ops:
  0.6 1.2 %copy-start = (f32[32,16,512]{2,1,0:T(8,128)S(1)}, f32[32,16,512]{2,1,0:T(8,128)}, u32[]{:S(2)}) copy-start(f32[32,16,512]{2,1,0:T(8,128)} %param.7) | copy-start | bytes 3145732
  1.9 0.9 %copy-start.1 = (f32[32,2,4,128]{3,2,1,0:T(4,128)S(1)}, f32[32,2,4,128]{3,2,1,0:T(4,128)}, u32[]{:S(2)}) copy-start(f32[32,2,4,128]{3,2,1,0:T(4,128)} %param.6) | copy-start | bytes 393220
  2.8 0.8 copy-start.2
  3.6 0.8 copy-start.3

commit v2 on v1

--- a/solution.py
+++ b/solution.py
@@ -13,16 +13,17 @@
 KT, IB, PM = 32, 16, 512
 NY, NZ = 8, 4
 CELLS = 1024
-SPLIT = 768
 F32, BF16 = jnp.float32, jnp.bfloat16
 
-AZ = 0
-AR = AZ + 3
-AL = AR + 16
-BR = AL + 16
-BL = BR + 4
-BZ = BL + 4
-NMSG = BZ + 24
+APIECES = [slice(0, 384), slice(384, 768)]
+BPIECE = slice(768, 1024)
+ZORDER = (2, 1, 3)
+OFF = [0, 0.8, 1.2, 0.8]
+NA = 35
+NB0 = NA * len(APIECES)
+NMSG = NB0 + 32
+
+SLOT = list(range(NY))
 
 
 def lanes_next(v):
@@ -41,16 +42,18 @@
     return hi, (x - hi.astype(F32)).astype(BF16)
 
 
-def kernel(u_ref, src_ref, a_ref, c_ref, po_ref, ro_ref,
-           ug, a_halo, c_hi, c_lo, faces, dinv, m_ref, uh_ref, ul_ref,
-           hs_send, hs_recv, out_u, src_m,
-           gs, gr, hss, hsr, cs, cr):
+def kernel(u_hbm, src_hbm, a_hbm, c_hbm, po_ref, ro_ref,
+           u_ref, src_ref, a_ref, c_ref,
+           ug, a_halo, c_st, faces, dinv, m_ref, u_st,
+           hs_send, hs_recv, src_m,
+           ls, gs, gr, hss, hsr, cs, cr):
     mode, space = lax.axis_index("mode"), lax.axis_index("space")
     ns = lax.axis_size("space")
     zh, y = mode // NY, lax.rem(mode, NY)
     left_s, right_s = lax.rem(space + ns - 1, ns), lax.rem(space + 1, ns)
     yr = zh * NY + lax.rem(y + 1, NY)
     yl = zh * NY + lax.rem(y + NY - 1, NY)
+    has_l, has_r = space > 0, space < ns - 1
 
     def at_z(q):
         return lax.rem(zh + q, NZ) * NY + y
@@ -64,9 +67,51 @@
     for target in (left_s, right_s):
         pl.semaphore_signal(barrier, inc=1, device_id={"mode": mode, "space": target}, device_id_type=MESH)
 
+    loads = [pltpu.make_async_copy(h, v, ls.at[n]) for n, (h, v) in enumerate(
+        ((u_hbm, u_ref), (a_hbm, a_ref), (c_hbm, c_ref), (src_hbm, src_ref)))]
+    for copy in loads:
+        copy.start()
+
+    def tile(s):
+        return slice(s * 128, (s + 1) * 128)
+
+    loads[0].wait()
     for s in range(8):
-        ug[0, mode, :, s * 128:(s + 1) * 128] = u_ref[:, s, :]
-        src_m[:, s * 128:(s + 1) * 128] = src_ref[:, s, :]
+        ug[0, mode, :, tile(s)] = u_ref[:, s, :]
+    loads[1].wait()
+
+    def own_faces(k, _):
+        a = a_ref[k]
+        a4 = pltpu.roll(a, 4, 0)
+        sub8 = lax.rem(lax.broadcasted_iota(jnp.int32, (8, 128), 0), 4)
+        ym = jnp.where(sub8 > 0, pltpu.roll(a, 1, 0), 0.0)
+        yp = jnp.where(sub8 < 3, pltpu.roll(a, 7, 0), 0.0)
+        for n, v in enumerate((a4, a4, ym, yp, lanes_prev(a), lanes_next(a))):
+            faces[n, k] = 0.5 * (a + v)
+        return 0
+
+    lax.fori_loop(0, KT, own_faces, 0, unroll=8)
+
+    loads[2].wait()
+    for r in range(8):
+        rows = slice(r * 64, (r + 1) * 64)
+        hi, lo = [], []
+        for q in range(NZ):
+            cols = pl.ds(pl.multiple_of(lax.rem(zh + q, NZ) * 128, 128), 128)
+            x = pltpu.roll(c_ref[rows, cols], lax.rem(NY - y, NY) * IB, 1)
+            h = x.astype(BF16).astype(F32)
+            hi.append(h)
+            lo.append(x - h)
+        for d in range(NY):
+            part = slice(d * IB, (d + 1) * IB)
+            h = jnp.concatenate([v[:, part] for v in hi], axis=1)
+            l = jnp.concatenate([v[:, part] for v in lo], axis=1)
+            c_st[SLOT[d], rows, 0:64] = h.astype(BF16)
+            c_st[SLOT[d], rows, 64:128] = h.astype(BF16)
+            c_st[SLOT[d], rows, 128:192] = l.astype(BF16)
+    loads[3].wait()
+    for s in range(8):
+        src_m[:, tile(s)] = src_ref[:, s, :]
     pl.semaphore_wait(barrier, 7)
 
     def coef_copy(side):
@@ -82,7 +127,21 @@
             send_sem=hss.at[it, side], recv_sem=hsr.at[it, side],
             device_id={"mode": mode, "space": target}, device_id_type=MESH)
 
-    acols, bcols = slice(0, SPLIT), slice(SPLIT, CELLS)
+    def mix(it, ds, first):
+        for n, d in enumerate(ds):
+            for q in range(NZ):
+                hi, lo = split_bf16(ug[it, block(q, d)])
+                base = n * 192 + q * IB
+                u_st[base:base + IB, :] = hi
+                u_st[base + 64:base + 64 + IB, :] = lo
+                u_st[base + 128:base + 128 + IB, :] = hi
+        for t in range(4):
+            cols = slice(t * 256, (t + 1) * 256)
+            acc = None
+            for n, d in enumerate(ds):
+                v = jnp.dot(c_st[SLOT[d % NY]], u_st[n * 192:(n + 1) * 192, cols], preferred_element_type=F32)
+                acc = v if acc is None else acc + v
+            m_ref[:, cols] = acc if first else m_ref[:, cols] + acc
 
     def gather(it):
         sent = []
@@ -101,82 +160,106 @@
         def arrive(number, b, cols):
             msg(number, b, cols, yr).wait_recv()
 
-        limit_r = [4, 3, 4, 3]
-        limit_l = [3, 4, 3, 4]
-
-        def a_right(q, t):
-            send(AR + q * 4 + t - 1, block(q, -(t - 1)), acols, yr)
-
-        def a_left(q, t):
-            send(AL + q * 4 + t - 1, block(q, t - 1), acols, yl)
+        limit_r, limit_l = [4, 3, 4, 3], [3, 4, 3, 4]
+
+        def a_right(p, q, t):
+            send(p * NA + 3 + q * 4 + t - 1, block(q, -(t - 1)), APIECES[p], yr)
+
+        def a_left(p, q, t):
+            send(p * NA + 19 + q * 4 + t - 1, block(q, t - 1), APIECES[p], yl)
 
         def b_z(d):
-            for q in (1, 2, 3):
-                send(BZ + (d % NY) * 3 + q - 1, block(0, d), bcols, at_z(q))
-
-        for q in (1, 3, 2):
-            send(AZ + q - 1, mode, acols, at_z(q))
-        send(BR + 0, mode, bcols, yr)
-        send(BL + 0, mode, bcols, yl)
-        a_right(0, 1)
-        a_left(0, 1)
+            for q in ZORDER:
+                send(NB0 + 8 + (d % NY) * 3 + q - 1, block(0, d), BPIECE, at_z(q))
+
+        def b_z_arrive(d):
+            for q in ZORDER:
+                arrive(NB0 + 8 + (d % NY) * 3 + q - 1, block(NZ - q, d), BPIECE)
+
+        def b_r(t):
+            send(NB0 + t - 1, block(0, -(t - 1)), BPIECE, yr)
+
+        def b_l(t):
+            send(NB0 + 4 + t - 1, block(0, t - 1), BPIECE, yl)
+
+        b_r(1)
+        b_l(1)
+        for p in range(len(APIECES)):
+            a_right(p, 0, 1)
+            a_left(p, 0, 1)
+            for q in ZORDER:
+                send(p * NA + q - 1, mode, APIECES[p], at_z(q))
         b_z(0)
-        for q in (1, 3, 2):
-            arrive(AZ + q - 1, block(NZ - q, 0), acols)
-            a_right(NZ - q, 1)
-            a_left(NZ - q, 1)
-        for t in (1, 2, 3, 4):
-            if t <= 4:
-                arrive(BR + t - 1, block(0, -t), bcols)
+        if it == 0:
+            coef_copy(0).start()
+            coef_copy(1).start()
+        events = [(2.55, 'm', 0, 0, 1), (3.55, 'm', 0, 0, 2), (4.55, 'm', 0, 0, 3)]
+        if it == 0:
+            events.append((2.6, 'h', 0, 0, 0))
+        for p in range(len(APIECES)):
+            for q in ZORDER:
+                events.append((OFF[NZ - q] + 0.3 * p + 0.01 * ZORDER.index(q), 'z', p, q, 0))
+            for q in range(NZ):
+                for t in range(1, 5):
+                    if t <= limit_r[q]:
+                        events.append((OFF[q] + 0.3 * p + t, 'r', p, q, t))
+                    if t <= limit_l[q]:
+                        events.append((OFF[q] + 0.3 * p + t + 0.001, 'l', p, q, t))
+        for t in range(1, 5):
+            events.append((t - 0.002, 'br', 0, 0, t))
+            if t < 4:
+                events.append((t - 0.001, 'bl', 0, 0, t))
+        for _, kind, p, q, t in sorted(events):
+            if kind == 'z':
+                arrive(p * NA + q - 1, block(NZ - q, 0), APIECES[p])
+                a_right(p, NZ - q, 1)
+                a_left(p, NZ - q, 1)
+            elif kind == 'r':
+                arrive(p * NA + 3 + q * 4 + t - 1, block(q, -t), APIECES[p])
+                if t < limit_r[q]:
+                    a_right(p, q, t + 1)
+            elif kind == 'l':
+                arrive(p * NA + 19 + q * 4 + t - 1, block(q, t), APIECES[p])
+                if t < limit_l[q]:
+                    a_left(p, q, t + 1)
+            elif kind == 'br':
+                arrive(NB0 + t - 1, block(0, -t), BPIECE)
                 if t < 4:
-                    send(BR + t, block(0, -t), bcols, yr)
+                    b_r(t + 1)
                 b_z(-t)
-            if t <= 3:
-                arrive(BL + t - 1, block(0, t), bcols)
+            elif kind == 'bl':
+                arrive(NB0 + 4 + t - 1, block(0, t), BPIECE)
                 if t < 3:
-                    send(BL + t, block(0, t), bcols, yl)
+                    b_l(t + 1)
                 b_z(t)
-            for q in (0, 3, 1, 2):
-                if t <= limit_r[q]:
-                    arrive(AR + q * 4 + t - 1, block(q, -t), acols)
-                    if t < limit_r[q]:
-                        a_right(q, t + 1)
-                if t <= limit_l[q]:
-                    arrive(AL + q * 4 + t - 1, block(q, t), acols)
-                    if t < limit_l[q]:
-                        a_left(q, t + 1)
-        for d in range(NY):
-            for q in (1, 2, 3):
-                arrive(BZ + d * 3 + q - 1, block(NZ - q, d), bcols)
+            elif kind == 'h':
+                prepare()
+            elif t == 1:
+                b_z_arrive(0)
+                mix(it, (0,), True)
+            else:
+                b_z_arrive(t - 1)
+                b_z_arrive(1 - t)
+                mix(it, (t - 1, 1 - t), False)
+        b_z_arrive(3)
+        b_z_arrive(-3)
+        mix(it, (3, -3), False)
+        b_z_arrive(4)
+        mix(it, (4,), False)
         return sent
 
+    sub = lax.broadcasted_iota(jnp.int32, (8, 128), 0)
+    ysub = lax.rem(sub, 4)
+    plane0 = sub < 4
+
     def prepare():
-        for r in range(8):
-            rows = slice(r * 64, (r + 1) * 64)
-            hi, lo = split_bf16(c_ref[rows, :])
-            c_hi[rows, :] = hi
-            c_lo[rows, :] = lo
         coef_copy(0).wait_recv()
         coef_copy(1).wait_recv()
-        sub = lax.broadcasted_iota(jnp.int32, (8, 128), 0)
-        ysub = lax.rem(sub, 4)
-        plane0 = sub < 4
-        has_l, has_r = space > 0, space < ns - 1
-
-        def one(k, _):
-            a = a_ref[k]
-            al = jnp.where(has_l, a_halo[0, k], 0.0)
-            ar = jnp.where(has_r, a_halo[1, k], 0.0)
-            a4 = pltpu.roll(a, 4, 0)
-            xm = jnp.where(plane0, pltpu.roll(al, 4, 0), a4)
-            xp = jnp.where(plane0, a4, pltpu.roll(ar, 4, 0))
-            ym = jnp.where(ysub > 0, pltpu.roll(a, 1, 0), 0.0)
-            yp = jnp.where(ysub < 3, pltpu.roll(a, 7, 0), 0.0)
-            for n, v in enumerate((xm, xp, ym, yp, lanes_prev(a), lanes_next(a))):
-                faces[n, k] = 0.5 * (a + v)
-            return 0
-
-        lax.fori_loop(0, KT, one, 0)
+        for k in range(KT):
+            al = jnp.where(has_l, a_halo[0, k, 4:8, :], 0.0)
+            ar = jnp.where(has_r, a_halo[1, k, 0:4, :], 0.0)
+            faces[0, k, 0:4, :] = 0.5 * (a_ref[k, 0:4, :] + al)
+            faces[1, k, 4:8, :] = 0.5 * (a_ref[k, 4:8, :] + ar)
 
         def face_sum(a, x_nb):
             total = x_nb
@@ -193,41 +276,17 @@
         dinv[1] = DAMP / face_sum(al, a4 + al4)
         dinv[2] = DAMP / face_sum(ar, a4 + ar4)
 
-    def mixed(it):
-        for r in range(8):
-            x = ug[it, r * 4:(r + 1) * 4].reshape(64, CELLS)
-            hi, lo = split_bf16(x)
-            uh_ref[r * 64:(r + 1) * 64, :] = hi
-            ul_ref[r * 64:(r + 1) * 64, :] = lo
-        for t in range(4):
-            cols = slice(t * 256, (t + 1) * 256)
-            uh, ul = uh_ref[:, cols], ul_ref[:, cols]
-            acc = jnp.dot(c_hi[...], uh, preferred_element_type=F32)
-            acc += jnp.dot(c_hi[...], ul, preferred_element_type=F32)
-            acc += jnp.dot(c_lo[...], uh, preferred_element_type=F32)
-            m_ref[:, cols] = acc
-
     def sums(s):
-        def one(k, acc):
-            m = m_ref[pl.ds(pl.multiple_of(k * IB, IB), IB), s * 128:(s + 1) * 128]
-            return tuple(acc[n] + faces[n, k, s:s + 1, :] * m for n in range(6))
-
-        zero = jnp.zeros((IB, 128), F32)
-        return lax.fori_loop(0, KT, one, (zero,) * 6, unroll=4)
-
-    def tile(s):
-        return slice(s * 128, (s + 1) * 128)
-
-    coef_copy(0).start()
-    coef_copy(1).start()
+        acc = None
+        for k in range(KT):
+            m = m_ref[k * IB:(k + 1) * IB, tile(s)]
+            new = [faces[n, k, s:s + 1, :] * m for n in range(6)]
+            acc = new if acc is None else [a + b for a, b in zip(acc, new)]
+        return acc
+
     sent = []
-    has_l = space > 0
-    has_r = space < ns - 1
     for it in range(ITERS):
         sent += gather(it)
-        if it == 0:
-            prepare()
-        mixed(it)
         S = [sums(s) for s in range(8)]
         own = [ug[it, mode, :, tile(s)] for s in range(8)]
         part = []
@@ -288,28 +347,30 @@
 
 
 def on_device(pressure, source, coefficients, coupling):
-    vmem = pl.BlockSpec(memory_space=pltpu.VMEM)
+    vmem, hbm = pl.BlockSpec(memory_space=pltpu.VMEM), pl.BlockSpec(memory_space=pltpu.HBM)
     shape = jax.ShapeDtypeStruct((IB, 8, 128), F32)
     dma = pltpu.SemaphoreType.DMA
     out = pl.pallas_call(
         kernel,
         out_shape=(shape, shape),
-        in_specs=[vmem] * 4,
+        in_specs=[hbm] * 4,
         out_specs=(vmem, vmem),
         scratch_shapes=[
+            pltpu.VMEM((IB, 8, 128), F32),
+            pltpu.VMEM((IB, 8, 128), F32),
+            pltpu.VMEM((KT, 8, 128), F32),
+            pltpu.VMEM((PM, PM), F32),
             pltpu.VMEM((ITERS, PM // IB, IB, CELLS), F32),
             pltpu.VMEM((2, KT, 8, 128), F32),
-            pltpu.VMEM((PM, PM), BF16),
-            pltpu.VMEM((PM, PM), BF16),
+            pltpu.VMEM((NY, PM, 192), BF16),
             pltpu.VMEM((6, KT, 8, 128), F32),
             pltpu.VMEM((3, 8, 128), F32),
             pltpu.VMEM((PM, CELLS), F32),
-            pltpu.VMEM((PM, CELLS), BF16),
-            pltpu.VMEM((PM, CELLS), BF16),
+            pltpu.VMEM((384, CELLS), BF16),
             pltpu.VMEM((ITERS, 2, IB, CELLS), F32),
             pltpu.VMEM((ITERS, 2, IB, CELLS), F32),
             pltpu.VMEM((IB, CELLS), F32),
-            pltpu.VMEM((IB, CELLS), F32),
+            dma((4,)),
             dma((ITERS, NMSG)),
             dma((ITERS, NMSG)),
             dma((ITERS, 2)),
@@ -318,7 +379,7 @@
             dma((2,)),
         ],
         compiler_params=pltpu.CompilerParams(
-            collective_id=0, has_side_effects=True, vmem_limit_bytes=40 * 1024 * 1024),
+            collective_id=0, has_side_effects=True, vmem_limit_bytes=66_000_000),
     )(pressure.reshape(IB, 8, 128), source.reshape(IB, 8, 128),
       coefficients.reshape(KT, 8, 128), coupling.reshape(PM, PM))
     return tuple(o.reshape(IB, 2, 4, 128) for o in out)

time: 89.8 us -> 82.7 us (0.921); the launches traced: 88.1 us -> 82.5 us
  local copies, waits for them, and re-layouts: 5.06 us -> 2.14 us
  Pallas kernels: 82.4 us -> 79.7 us
    unnamed x10 -> x4, local copies, waits for them, and re-layouts: 5.06 us -> 2.14 us
    pallas_call x1, Pallas kernels: 82.4 us -> 79.7 us  [on_device(): pl.pallas_call(kernel, out_shape=(shape, shape), in_specs=[hbm] * 4, out_...]
where the time goes in v2:
time: 82.7 us; the launch traced here: 82.5 us
  Pallas kernels  79.7 us (96%)
  local copies, waits for them, and re-layouts  2.14 us (3%)
    pallas_call x1, Pallas kernels, on_device(): pl.pallas_call(kernel, out_shape=(shape, shape), in_specs=[hbm] * 4, out_...  79.7 us
    unnamed x4, local copies, waits for them, and re-layouts  2.14 us

profile of v2, /device:TPU:1, one launch (start us, length us, event | category | flops | bytes accessed | tf_op | source)
XLA Modules:
  0.0 82.5 jit_solution(13112582619170787725)
XLA Ops:
  0.6 79.7 %shard_map.59 = (f32[16,8,128]{2,1,0:T(8,128)}, f32[16,8,128]{2,1,0:T(8,128)}) custom-call(f32[16,8,128]{2,1,0:T(8,128)} %bitcast.8, f32[16,8,128]{2,1,0:T(8,128)} %bitcast.9, f32[32,8,128]{2,1,0:T(8,128)} %bitcast.7, f32[512,512]{1,0:T(8,128)} %bitcast.6), custom_call_target="tpu_custom_call" | custom-call | tf_op jit(solution)/shard_map/pallas_call | solution.py:353
  80.4 0.0 copy-start
  80.4 1.5 %copy.8 = f32[16,2,4,128]{3,2,1,0:T(4,128)} copy(f32[16,2,4,128]{3,2,1,0:T(4,128)} %bitcast.11) | data formatting | bytes 131072
  81.9 0.0 copy-done
  81.9 0.6 copy.9
Async XLA Ops:
  80.4 1.5 %copy-start = (f32[16,8,128]{2,1,0:T(8,128)S(1)}, f32[16,8,128]{2,1,0:T(8,128)}, u32[]{:S(2)}) copy-start(f32[16,8,128]{2,1,0:T(8,128)} %get-tuple-element.5) | copy-start | bytes 196612

commit v3 on v2

--- a/solution.py
+++ b/solution.py
@@ -127,21 +127,33 @@
             send_sem=hss.at[it, side], recv_sem=hsr.at[it, side],
             device_id={"mode": mode, "space": target}, device_id_type=MESH)
 
-    def mix(it, ds, first):
+    def stage(it, ds, cols):
         for n, d in enumerate(ds):
             for q in range(NZ):
-                hi, lo = split_bf16(ug[it, block(q, d)])
+                hi, lo = split_bf16(ug[it, block(q, d), :, cols])
                 base = n * 192 + q * IB
-                u_st[base:base + IB, :] = hi
-                u_st[base + 64:base + 64 + IB, :] = lo
-                u_st[base + 128:base + 128 + IB, :] = hi
+                u_st[base:base + IB, cols] = hi
+                u_st[base + 64:base + 64 + IB, cols] = lo
+                u_st[base + 128:base + 128 + IB, cols] = hi
+
+    def product(ds, cols):
+        acc = None
+        for n, d in enumerate(ds):
+            v = jnp.dot(c_st[SLOT[d % NY]], u_st[n * 192:(n + 1) * 192, cols], preferred_element_type=F32)
+            acc = v if acc is None else acc + v
+        return acc
+
+    def mix(it, ds, first):
+        stage(it, ds, slice(0, CELLS))
         for t in range(4):
             cols = slice(t * 256, (t + 1) * 256)
-            acc = None
-            for n, d in enumerate(ds):
-                v = jnp.dot(c_st[SLOT[d % NY]], u_st[n * 192:(n + 1) * 192, cols], preferred_element_type=F32)
-                acc = v if acc is None else acc + v
+            acc = product(ds, cols)
             m_ref[:, cols] = acc if first else m_ref[:, cols] + acc
+
+    def last(it, cols):
+        stage(it, (4,), cols)
+        m_ref[:, cols] = m_ref[:, cols] + product((4,), cols)
+        return [sums(s) for s in range(cols.start // 128, cols.stop // 128)]
 
     def gather(it):
         sent = []
@@ -193,7 +205,8 @@
         if it == 0:
             coef_copy(0).start()
             coef_copy(1).start()
-        events = [(2.55, 'm', 0, 0, 1), (3.55, 'm', 0, 0, 2), (4.55, 'm', 0, 0, 3)]
+        events = [(2.55, 'm', 0, 0, 1), (3.55, 'm', 0, 0, 2), (4.55, 'm', 0, 0, 3), (4.79, 'm', 0, 0, 4)]
+        face_sums = []
         if it == 0:
             events.append((2.6, 'h', 0, 0, 0))
         for p in range(len(APIECES)):
@@ -201,10 +214,12 @@
                 events.append((OFF[NZ - q] + 0.3 * p + 0.01 * ZORDER.index(q), 'z', p, q, 0))
             for q in range(NZ):
                 for t in range(1, 5):
+                    w = OFF[q] + 0.3 * p + t if t < 4 else 5 + p + 0.1 * OFF[q]
                     if t <= limit_r[q]:
-                        events.append((OFF[q] + 0.3 * p + t, 'r', p, q, t))
+                        events.append((w, 'r', p, q, t))
                     if t <= limit_l[q]:
-                        events.append((OFF[q] + 0.3 * p + t + 0.001, 'l', p, q, t))
+                        events.append((w + 0.001, 'l', p, q, t))
+            events.append((5.5 + p, 's', p, 0, 0))
         for t in range(1, 5):
             events.append((t - 0.002, 'br', 0, 0, t))
             if t < 4:
@@ -234,6 +249,8 @@
                 b_z(t)
             elif kind == 'h':
                 prepare()
+            elif kind == 's':
+                face_sums += last(it, APIECES[p])
             elif t == 1:
                 b_z_arrive(0)
                 mix(it, (0,), True)
@@ -241,12 +258,9 @@
                 b_z_arrive(t - 1)
                 b_z_arrive(1 - t)
                 mix(it, (t - 1, 1 - t), False)
-        b_z_arrive(3)
-        b_z_arrive(-3)
-        mix(it, (3, -3), False)
         b_z_arrive(4)
-        mix(it, (4,), False)
-        return sent
+        face_sums += last(it, BPIECE)
+        return sent, face_sums
 
     sub = lax.broadcasted_iota(jnp.int32, (8, 128), 0)
     ysub = lax.rem(sub, 4)
@@ -286,8 +300,8 @@
 
     sent = []
     for it in range(ITERS):
-        sent += gather(it)
-        S = [sums(s) for s in range(8)]
+        copies, S = gather(it)
+        sent += copies
         own = [ug[it, mode, :, tile(s)] for s in range(8)]
         part = []
         for s in range(8):

time: 82.7 us -> 80.4 us (0.972)
  Pallas kernels: 79.7 us -> 77.4 us
    pallas_call x1, Pallas kernels: 79.7 us -> 77.4 us  [on_device(): pl.pallas_call(kernel, out_shape=(shape, shape), in_specs=[hbm] * 4, out_...]
where the time goes in v3:
time: 80.4 us; the launch traced here: 80.2 us
  Pallas kernels  77.4 us (96%)
  local copies, waits for them, and re-layouts  2.14 us (3%)
    pallas_call x1, Pallas kernels, on_device(): pl.pallas_call(kernel, out_shape=(shape, shape), in_specs=[hbm] * 4, out_...  77.4 us
    unnamed x4, local copies, waits for them, and re-layouts  2.14 us

profile of v3, /device:TPU:1, one launch (start us, length us, event | category | flops | bytes accessed | tf_op | source)
XLA Modules:
  0.0 80.2 jit_solution(5691573283111250023)
XLA Ops:
  0.6 77.4 %shard_map.59 = (f32[16,8,128]{2,1,0:T(8,128)}, f32[16,8,128]{2,1,0:T(8,128)}) custom-call(f32[16,8,128]{2,1,0:T(8,128)} %bitcast.8, f32[16,8,128]{2,1,0:T(8,128)} %bitcast.9, f32[32,8,128]{2,1,0:T(8,128)} %bitcast.7, f32[512,512]{1,0:T(8,128)} %bitcast.6), custom_call_target="tpu_custom_call" | custom-call | tf_op jit(solution)/shard_map/pallas_call | solution.py:367
  78.1 0.0 copy-start
  78.1 1.5 %copy.8 = f32[16,2,4,128]{3,2,1,0:T(4,128)} copy(f32[16,2,4,128]{3,2,1,0:T(4,128)} %bitcast.11) | data formatting | bytes 131072
  79.6 0.0 copy-done
  79.6 0.6 copy.9
Async XLA Ops:
  78.1 1.5 %copy-start = (f32[16,8,128]{2,1,0:T(8,128)S(1)}, f32[16,8,128]{2,1,0:T(8,128)}, u32[]{:S(2)}) copy-start(f32[16,8,128]{2,1,0:T(8,128)} %get-tuple-element.5) | copy-start | bytes 196612

commit v4 on v3

--- a/solution.py
+++ b/solution.py
@@ -360,6 +360,11 @@
             halo_copy(it, side).wait_send()
 
 
+def hand_on(a_ref, b_ref, c_ref, d_ref):
+    c_ref[...] = a_ref[...]
+    d_ref[...] = b_ref[...]
+
+
 def on_device(pressure, source, coefficients, coupling):
     vmem, hbm = pl.BlockSpec(memory_space=pltpu.VMEM), pl.BlockSpec(memory_space=pltpu.HBM)
     shape = jax.ShapeDtypeStruct((IB, 8, 128), F32)
@@ -396,6 +401,8 @@
             collective_id=0, has_side_effects=True, vmem_limit_bytes=66_000_000),
     )(pressure.reshape(IB, 8, 128), source.reshape(IB, 8, 128),
       coefficients.reshape(KT, 8, 128), coupling.reshape(PM, PM))
+    out = pl.pallas_call(
+        hand_on, out_shape=(shape, shape), in_specs=[vmem] * 2, out_specs=(vmem, vmem))(*out)
     return tuple(o.reshape(IB, 2, 4, 128) for o in out)
 
 

time: 80.4 us -> 79.8 us (level)
  local copies, waits for them, and re-layouts: 2.14 us -> 0 us
  Pallas kernels: 77.4 us -> 79 us
    unnamed x4 -> x0, local copies, waits for them, and re-layouts: 2.14 us -> none
    pallas_call x0 -> x1, Pallas kernels: none -> 1.53 us  [on_device(): pl.pallas_call(hand_on, out_shape=(shape, shape), in_specs=[vmem] * 2, ou...]
where the time goes in v4:
time: 79.8 us; the launch traced here: 79.6 us
  Pallas kernels  79 us (99%)
    pallas_call x1, Pallas kernels, on_device(): pl.pallas_call(kernel, out_shape=(shape, shape), in_specs=[hbm] * 4, out_...  77.4 us

profile of v4, /device:TPU:1, one launch (start us, length us, event | category | flops | bytes accessed | tf_op | source)
XLA Modules:
  0.0 79.6 jit_solution(15473434528432492226)
XLA Ops:
  0.6 77.4 %shard_map.59 = (f32[16,8,128]{2,1,0:T(8,128)}, f32[16,8,128]{2,1,0:T(8,128)}) custom-call(f32[16,8,128]{2,1,0:T(8,128)} %bitcast.8, f32[16,8,128]{2,1,0:T(8,128)} %bitcast.9, f32[32,8,128]{2,1,0:T(8,128)} %bitcast.7, f32[512,512]{1,0:T(8,128)} %bitcast.6), custom_call_target="tpu_custom_call" | custom-call | tf_op jit(solution)/shard_map/pallas_call | solution.py:372
  78.1 1.5 %shard_map.60 = (f32[16,8,128]{2,1,0:T(8,128)}, f32[16,8,128]{2,1,0:T(8,128)}) custom-call(f32[16,8,128]{2,1,0:T(8,128)} %get-tuple-element.6.a_ref, f32[16,8,128]{2,1,0:T(8,128)} %get-tuple-element.7.b_ref), custom_call_target="tpu_custom_call" | custom-call | tf_op jit(solution)/shard_map/pallas_call | solution.py:404
